TPU v7x, 32 devices: a whole 2x2x4 slice. The times are simulated.
32 devices in a mesh: gx: 2 (over core), gy: 4 (over y, x), ma: 4 (over z).
Axes of the slice: x: 2, y: 2, z: 4, core: 2. Of those that a mesh axis runs over, the one named last changes fastest.
Arguments:
- object_field: float32 [2, 256, 1024], P(None, 'gx', 'gy'), may hold values from -5 to 5
- probe_modes: float32 [8, 2, 256, 256], P('ma'), may hold values from -1.5 to 1.5
- measured: float32 [2, 4, 2, 256, 256], P('gx', 'gy'), may hold values from 0.1 to 4
- positions: int32 [2, 4, 2, 2], P('gx', 'gy'), may hold values from 0 to 255, as said below
- slot_counts: int32 [2, 4], P('gx', 'gy'), may hold values from 1 to 2, as said below
Outputs:
- updated_object: float32 [2, 256, 1024], P(None, 'gx', 'gy')
Inputs may be any that keep to these rules, and one draw needn't show every extreme that they name: positions[a, b, s] holds a row 0 to 127 and a column 0 to 255 of tile (a, b); slots s >= slot_counts[a, b] are unused. `slot_counts`: some tile uses all 2 slots.
All inputs are finite; a program needn't handle non-finite values.
Results may differ from a plain program's by a relative error of at most 0.0023.
Values sent between devices are 32-bit elements; how exact they have to be, the bound alone decides.
A program may use at most 64 MiB of HBM per device.

v0:
```python
import math
import jax
import jax.numpy as jnp
from jax import lax
from jax.sharding import PartitionSpec as P

OUTER = 2
DAMPING = 1.0


def padded_2(block, sides, width):
    for axis, dim in sides:
        count = lax.axis_size(axis)
        forward = [(i, i + 1) for i in range(count - 1)]
        backward = [(target, source) for source, target in forward]
        low = lax.ppermute(
            lax.slice_in_dim(block, block.shape[dim] - width, None, axis=dim), axis, forward
        )
        high = lax.ppermute(lax.slice_in_dim(block, 0, width, axis=dim), axis, backward)
        block = jnp.concatenate([low, block, high], axis=dim)
    return block


def dft_tables(patch_width):
    ladder = jnp.arange(patch_width, dtype=jnp.int32)
    phases = ladder[:, None] * ladder[None, :] % patch_width
    angles = phases.astype(jnp.float32) * (2.0 * math.pi / patch_width)
    factor = 1.0 / math.sqrt(patch_width)
    real_part = jnp.cos(angles) * factor
    imag_part = -jnp.sin(angles) * factor
    table_one = jnp.concatenate(
        [jnp.concatenate([real_part, -imag_part], 1), jnp.concatenate([imag_part, real_part], 1)], 0
    ).astype(jnp.bfloat16)
    table_two = jnp.concatenate(
        [jnp.concatenate([real_part, imag_part], 1), jnp.concatenate([-imag_part, real_part], 1)], 0
    ).astype(jnp.bfloat16)
    return (table_one, table_two)


def forward_transform(wavefield, tables):
    patch_width = wavefield.shape[-1]
    halfway = jnp.einsum(
        "pqci,bcik->bpqk",
        tables[0].reshape(2, patch_width, 2, patch_width),
        wavefield,
        preferred_element_type=jnp.float32,
    ).astype(jnp.bfloat16)
    return jnp.einsum(
        "bcik,ckl->bil",
        halfway,
        tables[1].reshape(2, patch_width, 2 * patch_width),
        preferred_element_type=jnp.float32,
    )


def adjoint_transform(weighted, tables):
    patch_width = weighted.shape[1]
    halfway = jnp.einsum(
        "bik,kl->bil", weighted, tables[0], preferred_element_type=jnp.float32
    ).astype(jnp.bfloat16)
    return jnp.einsum(
        "pqci,bicl->bpql",
        tables[1].reshape(2, patch_width, 2, patch_width),
        halfway.reshape(halfway.shape[0], patch_width, 2, patch_width),
        preferred_element_type=jnp.float32,
    )


def exit_waves(probe_modes, windows):
    probe_real = probe_modes[None, :, 0]
    probe_imag = probe_modes[None, :, 1]
    window_real = windows[:, None, 0]
    window_imag = windows[:, None, 1]
    real_part = probe_real * window_real - probe_imag * window_imag
    imag_part = probe_real * window_imag + probe_imag * window_real
    wavefield = jnp.stack([real_part, imag_part], 2).astype(jnp.bfloat16)
    return wavefield.reshape(-1, 2, probe_modes.shape[-1], probe_modes.shape[-1])


def intensity_part(spectra, mode_count):
    patch_width = spectra.shape[1]
    grouped = spectra.reshape(-1, mode_count, patch_width, 2 * patch_width)
    squared = grouped * grouped
    return jnp.sum(squared[..., :patch_width] + squared[..., patch_width:], axis=1)


def change_part(spectra, moved_spectra, mode_count):
    patch_width = spectra.shape[1]
    grouped = spectra.reshape(-1, mode_count, patch_width, 2 * patch_width)
    shifted = moved_spectra.reshape(-1, mode_count, patch_width, 2 * patch_width)
    product = grouped * shifted
    return 2.0 * jnp.sum(product[..., :patch_width] + product[..., patch_width:], axis=1)


def mode_images(weights, spectra, probe_modes, tables):
    mode_count = probe_modes.shape[0]
    patch_width = probe_modes.shape[-1]
    doubled = jnp.concatenate([weights, weights], -1)
    grouped = spectra.reshape(-1, mode_count, patch_width, 2 * patch_width)
    weighted = (2.0 * grouped * doubled[:, None]).astype(jnp.bfloat16)
    returned = adjoint_transform(weighted.reshape(-1, patch_width, 2 * patch_width), tables)
    returned = returned.reshape(-1, mode_count, 2, patch_width, patch_width)
    probe_real = probe_modes[None, :, 0]
    probe_imag = probe_modes[None, :, 1]
    real_part = jnp.sum(probe_real * returned[:, :, 0] + probe_imag * returned[:, :, 1], axis=1)
    imag_part = jnp.sum(probe_real * returned[:, :, 1] - probe_imag * returned[:, :, 0], axis=1)
    return jnp.stack([real_part, imag_part], 1)


def fold_edges(widened, axis_dim, length, rim_width):
    middle = lax.slice_in_dim(widened, 2 * rim_width, 2 * rim_width + length, axis=axis_dim)
    low_rim = lax.slice_in_dim(widened, 0, rim_width, axis=axis_dim)
    high_rim = lax.slice_in_dim(
        widened, length + 3 * rim_width, length + 4 * rim_width, axis=axis_dim
    )
    low_pads = [(0, 0), (0, 0), (0, 0)]
    high_pads = [(0, 0), (0, 0), (0, 0)]
    low_pads[axis_dim] = (0, length - rim_width)
    high_pads[axis_dim] = (length - rim_width, 0)
    return middle + jnp.pad(low_rim, low_pads) + jnp.pad(high_rim, high_pads)


def shards(object_field, probe_modes, measured, positions, slot_counts):
    patch_width = probe_modes.shape[-1]
    mode_count = probe_modes.shape[0]
    rim_width = patch_width // 2
    tile_rows = object_field.shape[1]
    tile_cols = object_field.shape[2]
    slot_count = measured.shape[2]
    share_rows = tile_rows // lax.axis_size("ma")
    tables = dft_tables(patch_width)
    targets = measured[0, 0]
    centres = positions[0, 0]
    live_mask = (jnp.arange(slot_count, dtype=jnp.int32) < slot_counts[0, 0]).astype(jnp.float32)[
        :, None, None
    ]
    anchor = jnp.zeros((), jnp.int32)

    def spectra_of(current):
        padded = padded_2(current, (("gx", 1), ("gy", 2)), rim_width)
        windows = jnp.stack(
            [
                lax.dynamic_slice(
                    padded,
                    (anchor, centres[slot_index, 0], centres[slot_index, 1]),
                    (2, patch_width, patch_width),
                )
                for slot_index in range(slot_count)
            ],
            0,
        )
        return forward_transform(exit_waves(probe_modes, windows), tables)

    def mode_total(partial_value):
        return lax.psum(partial_value, "ma")

    def combine(folded):
        summed = lax.psum(folded, "ma")
        return summed

    def project(weights, spectra):
        pieces = mode_images(weights, spectra, probe_modes, tables)
        extended = jnp.zeros((2, tile_rows + patch_width, tile_cols + patch_width), jnp.float32)
        for slot_index in range(slot_count):
            corner = (anchor, centres[slot_index, 0], centres[slot_index, 1])
            extended = lax.dynamic_update_slice(
                extended,
                lax.dynamic_slice(extended, corner, (2, patch_width, patch_width))
                + pieces[slot_index],
                corner,
            )
        widened = padded_2(extended, (("gx", 1), ("gy", 2)), rim_width)
        folded = fold_edges(fold_edges(widened, 1, tile_rows, rim_width), 2, tile_cols, rim_width)
        result = combine(folded)
        return result

    def local_sum(first_vec, second_vec):
        first_vec = lax.dynamic_slice_in_dim(
            first_vec, lax.axis_index("ma") * share_rows, share_rows, 1
        )
        second_vec = lax.dynamic_slice_in_dim(
            second_vec, lax.axis_index("ma") * share_rows, share_rows, 1
        )
        return jnp.sum(first_vec * second_vec)

    current = object_field
    for outer_step in range(OUTER):
        spectra = spectra_of(current)
        misfit = live_mask * (mode_total(intensity_part(spectra, mode_count)) - targets)
        gradient = project(misfit, spectra)
        residual = -gradient
        direction = residual
        norm_now = lax.psum(local_sum(residual, residual), ("gx", "gy", "ma"))
        moved_spectra = spectra_of(direction)
        change = live_mask * mode_total(change_part(spectra, moved_spectra, mode_count))
        applied = project(change, spectra) + DAMPING * direction
        step_size = norm_now / lax.psum(local_sum(direction, applied), ("gx", "gy", "ma"))
        update = step_size * direction
        residual = residual - step_size * applied
        current = current + update
    return current


def solution(mesh):
    return jax.shard_map(
        shards,
        mesh=mesh,
        in_specs=(
            P(None, "gx", "gy"),
            P("ma", None, None, None),
            P("gx", "gy", None, None, None),
            P("gx", "gy", None, None),
            P("gx", "gy"),
        ),
        out_specs=P(None, "gx", "gy"),
        check_vma=False,
    )
```

profile of v0, /device:TPU:0, one launch (start us, length us, event | category | flops | bytes accessed | tf_op | source)
XLA Modules:
  0.0 797.4 jit_solution(15070351154825093424)
XLA Ops:
  6.5 2.5 collective-permute-start
  13.7 4.2 collective-permute-start.2
  31.0 6.3 collective-permute-done.3
  45.2 36.4 %all-reduce.15.cloned.1.call-done = f32[2,256,256]{2,1,0:T(8,128)} async-done(((f32[2,256,256]{2,1,0:T(8,128)}), f32[2,256,256]{2,1,0:T(8,128)}) %all-reduce.15.cloned.1.call-update) | async-done | bytes 524304 | tf_op jit(solution)/shard_map/psum | solution.py:155
  89.5 7.8 dynamic_update_slice.24
  99.3 8.2 %dynamic_update_slice.25 = f32[2,384,512]{1,2,0:T(8,128)S(1)} dynamic-update-slice(f32[2,384,512]{1,2,0:T(8,128)S(1)} %dynamic_update_slice.24, f32[2,256,256]{1,2,0:T(8,128)} %fusion.50, s32[]{:T(128)} %constant.15.clone.1, s32[]{:T(128)S(6)} %select_n.33, s32[]{:T(128)S(6)} %select_n.34) | dynamic-update-slice | bytes 1048580 | tf_op jit(solution)/shard_map/dynamic_update_slice | solution.py:166
  110.4 2.3 collective-permute-done.5
  112.8 3.3 collective-permute-start.6
  117.4 12.9 %collective-permute-done.6 = f32[2,640,128]{1,2,0:T(8,128)S(1)} collective-permute-done((f32[2,640,128]{1,2,0:T(8,128)S(1)}, f32[2,640,128]{1,2,0:T(8,128)S(1)}, u32[]{:S(2)}, u32[]{:S(2)}) %collective-permute-start.6) | collective-permute-done | bytes 655392 | tf_op jit(solution)/shard_map/ppermute | solution.py:16
  130.4 16.7 %collective-permute-done.7 = f32[2,640,128]{1,2,0:T(8,128)S(1)} collective-permute-done((f32[2,640,128]{1,2,0:T(8,128)S(1)}, f32[2,640,128]{1,2,0:T(8,128)S(1)}, u32[]{:S(2)}, u32[]{:S(2)}) %collective-permute-start.7) | collective-permute-done | bytes 655392 | tf_op jit(solution)/shard_map/ppermute | solution.py:19
  148.6 33.7 %all-reduce.17.cloned.1.call-done = f32[2,128,256]{1,2,0:T(8,128)} async-done(((f32[2,128,256]{1,2,0:T(8,128)}), f32[2,128,256]{1,2,0:T(8,128)}) %all-reduce.17.cloned.1.call-update) | async-done | bytes 262160 | tf_op jit(solution)/shard_map/psum | solution.py:158
  185.9 2.1 collective-permute-done.9
  188.2 3.4 collective-permute-start.10
  193.0 7.2 collective-permute-done.10
  200.2 10.3 %collective-permute-done.11 = f32[2,384,128]{1,2,0:T(8,128)S(1)} collective-permute-done((f32[2,384,128]{1,2,0:T(8,128)S(1)}, f32[2,384,128]{1,2,0:T(8,128)S(1)}, u32[]{:S(2)}, u32[]{:S(2)}) %collective-permute-start.11) | collective-permute-done | bytes 393248 | tf_op jit(solution)/shard_map/ppermute | solution.py:19
  218.3 37.7 %all-reduce.19.cloned.1.call-done = f32[2,256,256]{2,1,0:T(8,128)} async-done(((f32[2,256,256]{2,1,0:T(8,128)}), f32[2,256,256]{2,1,0:T(8,128)}) %all-reduce.19.cloned.1.call-update) | async-done | bytes 524304 | tf_op jit(solution)/shard_map/psum | solution.py:155
  263.8 7.8 dynamic_update_slice.26
  273.6 8.2 %dynamic_update_slice.27 = f32[2,384,512]{1,2,0:T(8,128)S(1)} dynamic-update-slice(f32[2,384,512]{1,2,0:T(8,128)S(1)} %dynamic_update_slice.26, f32[2,256,256]{1,2,0:T(8,128)} %fusion.47, s32[]{:T(128)} %constant.15.clone.1, s32[]{:T(128)S(6)} %select_n.33, s32[]{:T(128)S(6)} %select_n.34) | dynamic-update-slice | bytes 1048580 | tf_op jit(solution)/shard_map/dynamic_update_slice | solution.py:166
  284.7 2.3 collective-permute-done.13
  287.2 3.3 collective-permute-start.14
  291.8 12.9 %collective-permute-done.14 = f32[2,640,128]{1,2,0:T(8,128)S(1)} collective-permute-done((f32[2,640,128]{1,2,0:T(8,128)S(1)}, f32[2,640,128]{1,2,0:T(8,128)S(1)}, u32[]{:S(2)}, u32[]{:S(2)}) %collective-permute-start.14) | collective-permute-done | bytes 655392 | tf_op jit(solution)/shard_map/ppermute | solution.py:16
  304.7 16.7 %collective-permute-done.15 = f32[2,640,128]{1,2,0:T(8,128)S(1)} collective-permute-done((f32[2,640,128]{1,2,0:T(8,128)S(1)}, f32[2,640,128]{1,2,0:T(8,128)S(1)}, u32[]{:S(2)}, u32[]{:S(2)}) %collective-permute-start.15) | collective-permute-done | bytes 655392 | tf_op jit(solution)/shard_map/ppermute | solution.py:19
  322.6 33.6 %all-reduce.21.cloned.1.call-done = f32[2,128,256]{1,2,0:T(8,128)} async-done(((f32[2,128,256]{1,2,0:T(8,128)}), f32[2,128,256]{1,2,0:T(8,128)}) %all-reduce.21.cloned.1.call-update) | async-done | bytes 262160 | tf_op jit(solution)/shard_map/psum | solution.py:158
  357.9 40.4 %all-reduce.5 = (f32[]{:T(128)}, f32[]{:T(128)}) all-reduce(f32[]{:T(128)} %get-tuple-element.16, f32[]{:T(128)} %get-tuple-element.15), channel_id=1, replica_groups=mesh['gx'=2,'gy'=4,'ma'=4] {'gx','gy','ma'}, use_global_device_ids=true, to_apply=%region_6.7 | all-reduce | flops 2 | bytes 16 | tf_op jit(solution)/shard_map/psum | solution.py:193
  402.3 2.1 collective-permute-done.17
  404.6 4.2 collective-permute-start.18
  410.1 7.3 collective-permute-done.18
  417.4 10.6 %collective-permute-done.19 = f32[2,384,128]{1,2,0:T(8,128)S(1)} collective-permute-done((f32[2,384,128]{1,2,0:T(8,128)S(1)}, f32[2,384,128]{1,2,0:T(8,128)S(1)}, u32[]{:S(2)}, u32[]{:S(2)}) %collective-permute-start.19) | collective-permute-done | bytes 393248 | tf_op jit(solution)/shard_map/ppermute | solution.py:19
  435.4 36.2 %all-reduce.23.cloned.1.call-done = f32[2,256,256]{2,1,0:T(8,128)} async-done(((f32[2,256,256]{2,1,0:T(8,128)}), f32[2,256,256]{2,1,0:T(8,128)}) %all-reduce.23.cloned.1.call-update) | async-done | bytes 524304 | tf_op jit(solution)/shard_map/psum | solution.py:155
  479.5 7.8 dynamic_update_slice.28
  489.3 8.2 %dynamic_update_slice.29 = f32[2,384,512]{1,2,0:T(8,128)S(1)} dynamic-update-slice(f32[2,384,512]{1,2,0:T(8,128)S(1)} %dynamic_update_slice.28, f32[2,256,256]{1,2,0:T(8,128)} %fusion.44, s32[]{:T(128)} %constant.15.clone.1, s32[]{:T(128)S(6)} %select_n.33, s32[]{:T(128)S(6)} %select_n.34) | dynamic-update-slice | bytes 1048580 | tf_op jit(solution)/shard_map/dynamic_update_slice | solution.py:166
  500.4 2.3 collective-permute-done.21
  502.8 3.3 collective-permute-start.22
  507.4 12.9 %collective-permute-done.22 = f32[2,640,128]{1,2,0:T(8,128)S(1)} collective-permute-done((f32[2,640,128]{1,2,0:T(8,128)S(1)}, f32[2,640,128]{1,2,0:T(8,128)S(1)}, u32[]{:S(2)}, u32[]{:S(2)}) %collective-permute-start.22) | collective-permute-done | bytes 655392 | tf_op jit(solution)/shard_map/ppermute | solution.py:16
  520.4 16.7 %collective-permute-done.23 = f32[2,640,128]{1,2,0:T(8,128)S(1)} collective-permute-done((f32[2,640,128]{1,2,0:T(8,128)S(1)}, f32[2,640,128]{1,2,0:T(8,128)S(1)}, u32[]{:S(2)}, u32[]{:S(2)}) %collective-permute-start.23) | collective-permute-done | bytes 655392 | tf_op jit(solution)/shard_map/ppermute | solution.py:19
  538.0 33.7 %all-reduce.25.cloned.1.call-done = f32[2,128,256]{1,2,0:T(8,128)} async-done(((f32[2,128,256]{1,2,0:T(8,128)}), f32[2,128,256]{1,2,0:T(8,128)}) %all-reduce.25.cloned.1.call-update) | async-done | bytes 262160 | tf_op jit(solution)/shard_map/psum | solution.py:158
  577.6 3.4 collective-permute-start.26
  582.3 7.3 collective-permute-done.26
  589.6 10.3 %collective-permute-done.27 = f32[2,384,128]{1,2,0:T(8,128)S(1)} collective-permute-done((f32[2,384,128]{1,2,0:T(8,128)S(1)}, f32[2,384,128]{1,2,0:T(8,128)S(1)}, u32[]{:S(2)}, u32[]{:S(2)}) %collective-permute-start.27) | collective-permute-done | bytes 393248 | tf_op jit(solution)/shard_map/ppermute | solution.py:19
  607.7 37.7 %all-reduce.27.cloned.1.call-done = f32[2,256,256]{2,1,0:T(8,128)} async-done(((f32[2,256,256]{2,1,0:T(8,128)}), f32[2,256,256]{2,1,0:T(8,128)}) %all-reduce.27.cloned.1.call-update) | async-done | bytes 524304 | tf_op jit(solution)/shard_map/psum | solution.py:155
  653.0 8.2 %dynamic_update_slice.30 = f32[2,384,512]{1,2,0:T(8,128)S(1)} dynamic-update-slice(f32[2,384,512]{1,2,0:T(8,128)S(1)} %broadcast.214, f32[2,256,256]{1,2,0:T(8,128)S(1)} %fusion.25, s32[]{:T(128)} %constant.15.clone.1, s32[]{:T(128)S(6)} %select_n.31, s32[]{:T(128)S(6)} %select_n.32) | dynamic-update-slice | bytes 1048580 | tf_op jit(solution)/shard_map/dynamic_update_slice | solution.py:166
  662.4 8.8 %dynamic_update_slice.31 = f32[2,384,512]{1,2,0:T(8,128)S(1)} dynamic-update-slice(f32[2,384,512]{1,2,0:T(8,128)S(1)} %dynamic_update_slice.30, f32[2,256,256]{1,2,0:T(8,128)S(1)} %fusion.41, s32[]{:T(128)} %constant.15.clone.1, s32[]{:T(128)S(6)} %select_n.33, s32[]{:T(128)S(6)} %select_n.34) | dynamic-update-slice | bytes 1048580 | tf_op jit(solution)/shard_map/dynamic_update_slice | solution.py:166
  674.2 2.3 collective-permute-done.29
  676.6 3.2 collective-permute-start.30
  681.1 12.9 %collective-permute-done.30 = f32[2,640,128]{1,2,0:T(8,128)S(1)} collective-permute-done((f32[2,640,128]{1,2,0:T(8,128)S(1)}, f32[2,640,128]{1,2,0:T(8,128)S(1)}, u32[]{:S(2)}, u32[]{:S(2)}) %collective-permute-start.30) | collective-permute-done | bytes 655392 | tf_op jit(solution)/shard_map/ppermute | solution.py:16
  694.1 16.9 %collective-permute-done.31 = f32[2,640,128]{1,2,0:T(8,128)S(1)} collective-permute-done((f32[2,640,128]{1,2,0:T(8,128)S(1)}, f32[2,640,128]{1,2,0:T(8,128)S(1)}, u32[]{:S(2)}, u32[]{:S(2)}) %collective-permute-start.31) | collective-permute-done | bytes 655392 | tf_op jit(solution)/shard_map/ppermute | solution.py:19
  712.0 33.7 %all-reduce.29.cloned.1.call-done = f32[2,128,256]{1,2,0:T(8,128)} async-done(((f32[2,128,256]{1,2,0:T(8,128)}), f32[2,128,256]{1,2,0:T(8,128)}) %all-reduce.29.cloned.1.call-update) | async-done | bytes 262160 | tf_op jit(solution)/shard_map/psum | solution.py:158
  747.6 40.4 %all-reduce.4 = (f32[]{:T(128)}, f32[]{:T(128)}) all-reduce(f32[]{:T(128)} %get-tuple-element.14, f32[]{:T(128)} %get-tuple-element.13), channel_id=1, replica_groups=mesh['gx'=2,'gy'=4,'ma'=4] {'gx','gy','ma'}, use_global_device_ids=true, to_apply=%region_20.21 | all-reduce | flops 2 | bytes 16 | tf_op jit(solution)/shard_map/psum | solution.py:193
  (248 shorter events, 120.0 us)
Async XLA Ops:
  6.5 75.1 %all-reduce.15.cloned.1.call-start = ((), (), s32[]{:S(2)}) async-start(), calls=%async_computation | async-start | bytes 1048576 | tf_op jit(solution)/shard_map/psum | solution.py:155
  6.5 5.2 collective-permute-start
  9.1 3.6 collective-permute-start.1
  13.7 17.3 %collective-permute-start.2 = (f32[2,384,128]{2,1,0:T(8,128)}, f32[2,384,128]{2,1,0:T(8,128)S(1)}, u32[]{:S(2)}, u32[]{:S(2)}) collective-permute-start(f32[2,384,128]{2,1,0:T(8,128)} %get-tuple-element.69), channel_id=1, source_target_pairs={{0,4},{4,8},{8,12},{1,5},{5,9},{9,13},{2,6},{6,10},{10,14},{3,7},{... | collective-permute-start | bytes 1179656 | tf_op jit(solution)/shard_map/ppermute | solution.py:16
  17.9 19.4 %collective-permute-start.3 = (f32[2,384,128]{2,1,0:T(8,128)}, f32[2,384,128]{2,1,0:T(8,128)}, u32[]{:S(2)}, u32[]{:S(2)}) collective-permute-start(f32[2,384,128]{2,1,0:T(8,128)} %get-tuple-element.70), channel_id=1, source_target_pairs={{4,0},{8,4},{12,8},{5,1},{9,5},{13,9},{6,2},{10,6},{14,10},{7,3},{... | collective-permute-start | bytes 1179656 | tf_op jit(solution)/shard_map/ppermute | solution.py:19
  28.3 10.1 %copy-start.18 = (bf16[512,512]{1,0:T(8,128)(2,1)}, bf16[512,512]{1,0:T(8,128)(2,1)S(1)}, u32[]{:S(2)}) copy-start(bf16[512,512]{1,0:T(8,128)(2,1)S(1)} %get-tuple-element.72) | copy-start | bytes 1572868
  28.4 11.2 %copy-start.27 = (bf16[2,256,2,256]{3,2,1,0:T(2,128)(2,1)}, bf16[2,256,2,256]{3,2,1,0:T(2,128)(2,1)S(1)}, u32[]{:S(2)}) copy-start(bf16[2,256,2,256]{3,2,1,0:T(2,128)(2,1)S(1)} %convert_element_type.132) | copy-start | bytes 1572868
  41.4 41.6 %copy-start = (f32[2,2,256,512,1]{3,2,4,1,0:T(8,128)}, f32[2,2,256,512,1]{3,2,4,1,0:T(8,128)S(1)}, u32[]{:S(2)}) copy-start(f32[2,2,256,512,1]{3,2,4,1,0:T(8,128)S(1)} %get-tuple-element.78) | copy-start | bytes 6291460
  42.5 139.8 %all-reduce.17.cloned.1.call-start = ((), (), s32[]{:S(2)}) async-start(), calls=%async_computation.1 | async-start | bytes 524288 | tf_op jit(solution)/shard_map/psum | solution.py:158
  107.6 2.8 collective-permute-start.4
  108.9 3.8 collective-permute-start.5
  112.8 17.5 %collective-permute-start.6 = (f32[2,640,128]{1,2,0:T(8,128)S(1)}, f32[2,640,128]{1,2,0:T(8,128)S(1)}, u32[]{:S(2)}, u32[]{:S(2)}) collective-permute-start(f32[2,640,128]{1,2,0:T(8,128)S(1)} %get-tuple-element.27), channel_id=1, source_target_pairs={{0,4},{4,8},{8,12},{1,5},{5,9},{9,13},{2,6},{6,10},{10,14},{3,7},{... | collective-permute-start | bytes 1966088 | tf_op jit(solution)/shard_map/ppermute | solution.py:16
  116.1 30.9 %collective-permute-start.7 = (f32[2,640,128]{1,2,0:T(8,128)S(1)}, f32[2,640,128]{1,2,0:T(8,128)S(1)}, u32[]{:S(2)}, u32[]{:S(2)}) collective-permute-start(f32[2,640,128]{1,2,0:T(8,128)S(1)} %get-tuple-element.28), channel_id=1, source_target_pairs={{4,0},{8,4},{12,8},{5,1},{9,5},{13,9},{6,2},{10,6},{14,10},{7,3},{... | collective-permute-start | bytes 1966088 | tf_op jit(solution)/shard_map/ppermute | solution.py:19
  148.5 107.5 %all-reduce.19.cloned.1.call-start = ((), (), s32[]{:S(2)}) async-start(), calls=%async_computation.2 | async-start | bytes 1048576 | tf_op jit(solution)/shard_map/psum | solution.py:155
  183.3 2.6 collective-permute-start.8
  184.6 3.4 collective-permute-start.9
  188.2 12.0 %collective-permute-start.10 = (f32[2,384,128]{1,2,0:T(8,128)S(1)}, f32[2,384,128]{1,2,0:T(8,128)S(1)}, u32[]{:S(2)}, u32[]{:S(2)}) collective-permute-start(f32[2,384,128]{1,2,0:T(8,128)S(1)} %get-tuple-element.67), channel_id=1, source_target_pairs={{0,4},{4,8},{8,12},{1,5},{5,9},{9,13},{2,6},{6,10},{10,14},{3,7},{... | collective-permute-start | bytes 1179656 | tf_op jit(solution)/shard_map/ppermute | solution.py:16
  191.6 19.0 %collective-permute-start.11 = (f32[2,384,128]{1,2,0:T(8,128)S(1)}, f32[2,384,128]{1,2,0:T(8,128)S(1)}, u32[]{:S(2)}, u32[]{:S(2)}) collective-permute-start(f32[2,384,128]{1,2,0:T(8,128)S(1)} %get-tuple-element.68), channel_id=1, source_target_pairs={{4,0},{8,4},{12,8},{5,1},{9,5},{13,9},{6,2},{10,6},{14,10},{7,3},{... | collective-permute-start | bytes 1179656 | tf_op jit(solution)/shard_map/ppermute | solution.py:19
  218.2 137.9 %all-reduce.21.cloned.1.call-start = ((), (), s32[]{:S(2)}) async-start(), calls=%async_computation.3 | async-start | bytes 524288 | tf_op jit(solution)/shard_map/psum | solution.py:158
  281.9 2.8 collective-permute-start.12
  283.3 3.8 collective-permute-start.13
  287.2 17.5 %collective-permute-start.14 = (f32[2,640,128]{1,2,0:T(8,128)S(1)}, f32[2,640,128]{1,2,0:T(8,128)S(1)}, u32[]{:S(2)}, u32[]{:S(2)}) collective-permute-start(f32[2,640,128]{1,2,0:T(8,128)S(1)} %get-tuple-element.25), channel_id=1, source_target_pairs={{0,4},{4,8},{8,12},{1,5},{5,9},{9,13},{2,6},{6,10},{10,14},{3,7},{... | collective-permute-start | bytes 1966088 | tf_op jit(solution)/shard_map/ppermute | solution.py:16
  290.5 30.9 %collective-permute-start.15 = (f32[2,640,128]{1,2,0:T(8,128)S(1)}, f32[2,640,128]{1,2,0:T(8,128)S(1)}, u32[]{:S(2)}, u32[]{:S(2)}) collective-permute-start(f32[2,640,128]{1,2,0:T(8,128)S(1)} %get-tuple-element.26), channel_id=1, source_target_pairs={{4,0},{8,4},{12,8},{5,1},{9,5},{13,9},{6,2},{10,6},{14,10},{7,3},{... | collective-permute-start | bytes 1966088 | tf_op jit(solution)/shard_map/ppermute | solution.py:19
  321.5 78.1 %copy-start.25 = (f32[2,128,256]{1,2,0:T(8,128)S(1)}, f32[2,128,256]{1,2,0:T(8,128)}, u32[]{:S(2)}) copy-start(f32[2,128,256]{1,2,0:T(8,128)} %all-reduce.17.cloned.1.call-done) | copy-start | bytes 786436
  322.4 149.3 %all-reduce.23.cloned.1.call-start = ((), (), s32[]{:S(2)}) async-start(), calls=%async_computation.4 | async-start | bytes 1048576 | tf_op jit(solution)/shard_map/psum | solution.py:155
  399.7 28.3 %copy-start.16 = (f32[2,128,256]{1,2,0:T(8,128)}, f32[2,128,256]{1,2,0:T(8,128)S(1)}, u32[]{:S(2)}) copy-start(f32[2,128,256]{1,2,0:T(8,128)S(1)} %multiply_add_fusion.1) | copy-start | bytes 786436
  399.7 2.6 collective-permute-start.16
  401.0 3.4 collective-permute-start.17
  404.6 12.8 %collective-permute-start.18 = (f32[2,384,128]{1,2,0:T(8,128)S(1)}, f32[2,384,128]{1,2,0:T(8,128)S(1)}, u32[]{:S(2)}, u32[]{:S(2)}) collective-permute-start(f32[2,384,128]{1,2,0:T(8,128)S(1)} %get-tuple-element.65), channel_id=1, source_target_pairs={{0,4},{4,8},{8,12},{1,5},{5,9},{9,13},{2,6},{6,10},{10,14},{3,7},{... | collective-permute-start | bytes 1179656 | tf_op jit(solution)/shard_map/ppermute | solution.py:16
  408.8 19.2 %collective-permute-start.19 = (f32[2,384,128]{1,2,0:T(8,128)S(1)}, f32[2,384,128]{1,2,0:T(8,128)S(1)}, u32[]{:S(2)}, u32[]{:S(2)}) collective-permute-start(f32[2,384,128]{1,2,0:T(8,128)S(1)} %get-tuple-element.66), channel_id=1, source_target_pairs={{4,0},{8,4},{12,8},{5,1},{9,5},{13,9},{6,2},{10,6},{14,10},{7,3},{... | collective-permute-start | bytes 1179656 | tf_op jit(solution)/shard_map/ppermute | solution.py:19
  434.0 39.0 %copy-start.2 = (f32[2,2,256,512,1]{3,2,4,1,0:T(8,128)}, f32[2,2,256,512,1]{3,2,4,1,0:T(8,128)S(1)}, u32[]{:S(2)}) copy-start(f32[2,2,256,512,1]{3,2,4,1,0:T(8,128)S(1)} %get-tuple-element.80) | copy-start | bytes 6291460
  435.1 136.6 %all-reduce.25.cloned.1.call-start = ((), (), s32[]{:S(2)}) async-start(), calls=%async_computation.5 | async-start | bytes 524288 | tf_op jit(solution)/shard_map/psum | solution.py:158
  497.6 2.8 collective-permute-start.20
  498.9 3.8 collective-permute-start.21
  502.8 17.5 %collective-permute-start.22 = (f32[2,640,128]{1,2,0:T(8,128)S(1)}, f32[2,640,128]{1,2,0:T(8,128)S(1)}, u32[]{:S(2)}, u32[]{:S(2)}) collective-permute-start(f32[2,640,128]{1,2,0:T(8,128)S(1)} %get-tuple-element.23), channel_id=1, source_target_pairs={{0,4},{4,8},{8,12},{1,5},{5,9},{9,13},{2,6},{6,10},{10,14},{3,7},{... | collective-permute-start | bytes 1966088 | tf_op jit(solution)/shard_map/ppermute | solution.py:16
  506.1 30.9 %collective-permute-start.23 = (f32[2,640,128]{1,2,0:T(8,128)S(1)}, f32[2,640,128]{1,2,0:T(8,128)S(1)}, u32[]{:S(2)}, u32[]{:S(2)}) collective-permute-start(f32[2,640,128]{1,2,0:T(8,128)S(1)} %get-tuple-element.24), channel_id=1, source_target_pairs={{4,0},{8,4},{12,8},{5,1},{9,5},{13,9},{6,2},{10,6},{14,10},{7,3},{... | collective-permute-start | bytes 1966088 | tf_op jit(solution)/shard_map/ppermute | solution.py:19
  538.0 107.5 %all-reduce.27.cloned.1.call-start = ((), (), s32[]{:S(2)}) async-start(), calls=%async_computation.6 | async-start | bytes 1048576 | tf_op jit(solution)/shard_map/psum | solution.py:155
  572.7 2.6 collective-permute-start.24
  574.0 3.4 collective-permute-start.25
  577.6 12.0 %collective-permute-start.26 = (f32[2,384,128]{1,2,0:T(8,128)S(1)}, f32[2,384,128]{1,2,0:T(8,128)S(1)}, u32[]{:S(2)}, u32[]{:S(2)}) collective-permute-start(f32[2,384,128]{1,2,0:T(8,128)S(1)} %get-tuple-element.63), channel_id=1, source_target_pairs={{0,4},{4,8},{8,12},{1,5},{5,9},{9,13},{2,6},{6,10},{10,14},{3,7},{... | collective-permute-start | bytes 1179656 | tf_op jit(solution)/shard_map/ppermute | solution.py:16
  581.0 19.0 %collective-permute-start.27 = (f32[2,384,128]{1,2,0:T(8,128)S(1)}, f32[2,384,128]{1,2,0:T(8,128)S(1)}, u32[]{:S(2)}, u32[]{:S(2)}) collective-permute-start(f32[2,384,128]{1,2,0:T(8,128)S(1)} %get-tuple-element.64), channel_id=1, source_target_pairs={{4,0},{8,4},{12,8},{5,1},{9,5},{13,9},{6,2},{10,6},{14,10},{7,3},{... | collective-permute-start | bytes 1179656 | tf_op jit(solution)/shard_map/ppermute | solution.py:19
  607.7 138.1 %all-reduce.29.cloned.1.call-start = ((), (), s32[]{:S(2)}) async-start(), calls=%async_computation.7 | async-start | bytes 524288 | tf_op jit(solution)/shard_map/psum | solution.py:158
  671.3 2.8 collective-permute-start.28
  672.7 3.8 collective-permute-start.29
  676.6 17.5 %collective-permute-start.30 = (f32[2,640,128]{1,2,0:T(8,128)S(1)}, f32[2,640,128]{1,2,0:T(8,128)S(1)}, u32[]{:S(2)}, u32[]{:S(2)}) collective-permute-start(f32[2,640,128]{1,2,0:T(8,128)S(1)} %get-tuple-element.21), channel_id=1, source_target_pairs={{0,4},{4,8},{8,12},{1,5},{5,9},{9,13},{2,6},{6,10},{10,14},{3,7},{... | collective-permute-start | bytes 1966088 | tf_op jit(solution)/shard_map/ppermute | solution.py:16
  679.8 31.2 %collective-permute-start.31 = (f32[2,640,128]{1,2,0:T(8,128)S(1)}, f32[2,640,128]{1,2,0:T(8,128)S(1)}, u32[]{:S(2)}, u32[]{:S(2)}) collective-permute-start(f32[2,640,128]{1,2,0:T(8,128)S(1)} %get-tuple-element.22), channel_id=1, source_target_pairs={{4,0},{8,4},{12,8},{5,1},{9,5},{13,9},{6,2},{10,6},{14,10},{7,3},{... | collective-permute-start | bytes 1966088 | tf_op jit(solution)/shard_map/ppermute | solution.py:19
  711.1 78.2 %copy-start.17 = (f32[2,128,256]{1,2,0:T(8,128)S(1)}, f32[2,128,256]{1,2,0:T(8,128)}, u32[]{:S(2)}) copy-start(f32[2,128,256]{1,2,0:T(8,128)} %copy-done.16) | copy-start | bytes 786436
  711.1 78.2 %copy-start.26 = (f32[2,128,256]{1,2,0:T(8,128)S(1)}, f32[2,128,256]{1,2,0:T(8,128)}, u32[]{:S(2)}) copy-start(f32[2,128,256]{1,2,0:T(8,128)} %all-reduce.25.cloned.1.call-done) | copy-start | bytes 786436
  (25 other events, 40.2 us)
Sparse Core Ops, SparseCore 0:
  42.6 38.9 all-reduce.14
  148.7 33.5 all-reduce.16
  218.4 37.6 all-reduce.18
  322.5 33.5 all-reduce.20
  435.2 36.3 all-reduce.22
  538.1 33.5 all-reduce.24
  607.8 37.6 all-reduce.26
  712.1 33.5 all-reduce.28
where the time goes:
time: 808 us; the launch traced here: 797 us
  waiting for transfers between devices  478 us (59%)
  local copies, waits for them, and re-layouts  94.4 us (12%)
  blocking collectives  80.8 us (10%)
  starting transfers between devices  61.5 us (8%)
  other arithmetic  40.6 us (5%)
  between operations  26.1 us (3%)
  matrix products  15.7 us (2%)
    psum x4, waiting for transfers between devices, mode_total(): return lax.psum(partial_value, 'ma')  148 us
    psum x4, waiting for transfers between devices, combine(): summed = lax.psum(folded, 'ma')  135 us
    ppermute x16, waiting for transfers between devices, padded_2(): lax.ppermute(lax.slice_in_dim(block, 0, width, axis=dim), axis, backward)  121 us
    psum x2, blocking collectives, shards(): norm_now = lax.psum(local_sum(residual, residual), ('gx', 'gy', 'ma'))  80.8 us
    ppermute x16, waiting for transfers between devices, padded_2(): lax.ppermute(lax.slice_in_dim(block, block.shape[dim] - width, None, axis...  74.3 us
    dynamic_update_slice x8, local copies, waits for them, and re-layouts, project(): lax.dynamic_update_slice(extended, lax.dynamic_slice(extended, corner, (2...  65.2 us
    ppermute x16, starting transfers between devices, padded_2(): lax.ppermute(lax.slice_in_dim(block, block.shape[dim] - width, None, axis...  40.1 us
    ppermute x16, starting transfers between devices, padded_2(): lax.ppermute(lax.slice_in_dim(block, 0, width, axis=dim), axis, backward)  20.8 us
  transfers between devices with their start and end apart: 40, of which 35 were waited for; matrix products, arithmetic and copies ran while one was open for 1% of the time, Pallas kernels for 0%

commit v1 on v0

--- a/solution.py
+++ b/solution.py
@@ -3,6 +3,7 @@
 import jax.numpy as jnp
 from jax import lax
 from jax.sharding import PartitionSpec as P
+from jax.lax import all_gather
 
 OUTER = 2
 DAMPING = 1.0
@@ -190,7 +191,7 @@
         gradient = project(misfit, spectra)
         residual = -gradient
         direction = residual
-        norm_now = lax.psum(local_sum(residual, residual), ("gx", "gy", "ma"))
+        norm_now = jnp.sum(all_gather(local_sum(residual, residual), ("gx", "gy", "ma")), 0)
         moved_spectra = spectra_of(direction)
         change = live_mask * mode_total(change_part(spectra, moved_spectra, mode_count))
         applied = project(change, spectra) + DAMPING * direction

time: 808 us -> 811 us (level)
    psum x2 -> x0, blocking collectives: 80.8 us -> none  [shards(): norm_now = lax.psum(local_sum(residual, residual), ('gx', 'gy', 'ma'))]
    unnamed x0 -> x2, blocking collectives: none -> 80.8 us
where the time goes in v1:
time: 811 us; the launch traced here: 800 us
  waiting for transfers between devices  479 us (59%)
  local copies, waits for them, and re-layouts  95.7 us (12%)
  blocking collectives  80.8 us (10%)
  starting transfers between devices  61.4 us (8%)
  other arithmetic  42 us (5%)
  between operations  25.8 us (3%)
  matrix products  15.7 us (2%)
    psum x4, waiting for transfers between devices, mode_total(): return lax.psum(partial_value, 'ma')  148 us
    psum x4, waiting for transfers between devices, combine(): summed = lax.psum(folded, 'ma')  135 us
    ppermute x16, waiting for transfers between devices, padded_2(): lax.ppermute(lax.slice_in_dim(block, 0, width, axis=dim), axis, backward)  121 us
    unnamed x2, blocking collectives  80.8 us
    ppermute x16, waiting for transfers between devices, padded_2(): lax.ppermute(lax.slice_in_dim(block, block.shape[dim] - width, None, axis...  74.3 us
    dynamic_update_slice x8, local copies, waits for them, and re-layouts, project(): lax.dynamic_update_slice(extended, lax.dynamic_slice(extended, corner, (2...  65.2 us
    ppermute x16, starting transfers between devices, padded_2(): lax.ppermute(lax.slice_in_dim(block, block.shape[dim] - width, None, axis...  40.1 us
    ppermute x16, starting transfers between devices, padded_2(): lax.ppermute(lax.slice_in_dim(block, 0, width, axis=dim), axis, backward)  20.8 us
  transfers between devices with their start and end apart: 40, of which 35 were waited for; matrix products, arithmetic and copies ran while one was open for 1% of the time, Pallas kernels for 0%

profile of v1, /device:TPU:0, one launch (start us, length us, event | category | flops | bytes accessed | tf_op | source)
XLA Modules:
  0.0 800.0 jit_solution(4215537090998334175)
XLA Ops:
  6.5 2.5 collective-permute-start
  13.7 4.2 collective-permute-start.2
  30.7 6.6 collective-permute-done.3
  45.2 36.4 %all-reduce.17.cloned.1.call-done = f32[2,256,256]{2,1,0:T(8,128)} async-done(((f32[2,256,256]{2,1,0:T(8,128)}), f32[2,256,256]{2,1,0:T(8,128)}) %all-reduce.17.cloned.1.call-update) | async-done | bytes 524304 | tf_op jit(solution)/shard_map/psum | solution.py:156
  89.5 7.8 dynamic_update_slice.24
  99.3 8.2 %dynamic_update_slice.25 = f32[2,384,512]{1,2,0:T(8,128)S(1)} dynamic-update-slice(f32[2,384,512]{1,2,0:T(8,128)S(1)} %dynamic_update_slice.24, f32[2,256,256]{1,2,0:T(8,128)} %fusion.50, s32[]{:T(128)} %constant.15.clone.1, s32[]{:T(128)S(6)} %select_n.33, s32[]{:T(128)S(6)} %select_n.34) | dynamic-update-slice | bytes 1048580 | tf_op jit(solution)/shard_map/dynamic_update_slice | solution.py:167
  110.5 2.3 collective-permute-done.5
  112.9 3.3 collective-permute-start.6
  117.5 12.9 %collective-permute-done.6 = f32[2,640,128]{1,2,0:T(8,128)S(1)} collective-permute-done((f32[2,640,128]{1,2,0:T(8,128)S(1)}, f32[2,640,128]{1,2,0:T(8,128)S(1)}, u32[]{:S(2)}, u32[]{:S(2)}) %collective-permute-start.6) | collective-permute-done | bytes 655392 | tf_op jit(solution)/shard_map/ppermute | solution.py:17
  130.4 16.7 %collective-permute-done.7 = f32[2,640,128]{1,2,0:T(8,128)S(1)} collective-permute-done((f32[2,640,128]{1,2,0:T(8,128)S(1)}, f32[2,640,128]{1,2,0:T(8,128)S(1)}, u32[]{:S(2)}, u32[]{:S(2)}) %collective-permute-start.7) | collective-permute-done | bytes 655392 | tf_op jit(solution)/shard_map/ppermute | solution.py:20
  148.7 33.7 %all-reduce.19.cloned.1.call-done = f32[2,128,256]{1,2,0:T(8,128)} async-done(((f32[2,128,256]{1,2,0:T(8,128)}), f32[2,128,256]{1,2,0:T(8,128)}) %all-reduce.19.cloned.1.call-update) | async-done | bytes 262160 | tf_op jit(solution)/shard_map/psum | solution.py:159
  186.0 2.1 collective-permute-done.9
  188.2 3.4 collective-permute-start.10
  193.1 7.2 collective-permute-done.10
  200.2 10.3 %collective-permute-done.11 = f32[2,384,128]{1,2,0:T(8,128)S(1)} collective-permute-done((f32[2,384,128]{1,2,0:T(8,128)S(1)}, f32[2,384,128]{1,2,0:T(8,128)S(1)}, u32[]{:S(2)}, u32[]{:S(2)}) %collective-permute-start.11) | collective-permute-done | bytes 393248 | tf_op jit(solution)/shard_map/ppermute | solution.py:20
  218.3 37.7 %all-reduce.21.cloned.1.call-done = f32[2,256,256]{2,1,0:T(8,128)} async-done(((f32[2,256,256]{2,1,0:T(8,128)}), f32[2,256,256]{2,1,0:T(8,128)}) %all-reduce.21.cloned.1.call-update) | async-done | bytes 524304 | tf_op jit(solution)/shard_map/psum | solution.py:156
  263.8 7.8 dynamic_update_slice.26
  273.7 8.2 %dynamic_update_slice.27 = f32[2,384,512]{1,2,0:T(8,128)S(1)} dynamic-update-slice(f32[2,384,512]{1,2,0:T(8,128)S(1)} %dynamic_update_slice.26, f32[2,256,256]{1,2,0:T(8,128)} %fusion.47, s32[]{:T(128)} %constant.15.clone.1, s32[]{:T(128)S(6)} %select_n.33, s32[]{:T(128)S(6)} %select_n.34) | dynamic-update-slice | bytes 1048580 | tf_op jit(solution)/shard_map/dynamic_update_slice | solution.py:167
  284.8 2.3 collective-permute-done.13
  287.2 3.3 collective-permute-start.14
  291.8 12.9 %collective-permute-done.14 = f32[2,640,128]{1,2,0:T(8,128)S(1)} collective-permute-done((f32[2,640,128]{1,2,0:T(8,128)S(1)}, f32[2,640,128]{1,2,0:T(8,128)S(1)}, u32[]{:S(2)}, u32[]{:S(2)}) %collective-permute-start.14) | collective-permute-done | bytes 655392 | tf_op jit(solution)/shard_map/ppermute | solution.py:17
  304.7 16.7 %collective-permute-done.15 = f32[2,640,128]{1,2,0:T(8,128)S(1)} collective-permute-done((f32[2,640,128]{1,2,0:T(8,128)S(1)}, f32[2,640,128]{1,2,0:T(8,128)S(1)}, u32[]{:S(2)}, u32[]{:S(2)}) %collective-permute-start.15) | collective-permute-done | bytes 655392 | tf_op jit(solution)/shard_map/ppermute | solution.py:20
  322.6 33.5 %all-reduce.23.cloned.1.call-done = f32[2,128,256]{1,2,0:T(8,128)} async-done(((f32[2,128,256]{1,2,0:T(8,128)}), f32[2,128,256]{1,2,0:T(8,128)}) %all-reduce.23.cloned.1.call-update) | async-done | bytes 262160 | tf_op jit(solution)/shard_map/psum | solution.py:159
  358.7 40.4 %all-reduce.7 = (f32[32]{0:T(128)S(1)}, f32[]{:T(128)}) all-reduce(f32[32]{0:T(128)S(1)} %dynamic-update-slice, f32[]{:T(128)} %get-tuple-element.15), channel_id=1, replica_groups=mesh['gx'=2,'gy'=4,'ma'=4] {'gx','gy','ma'}, use_global_device_ids=true, to_apply=%add.4 | all-reduce | flops 33 | bytes 264
  405.9 4.2 collective-permute-start.18
  411.5 7.3 collective-permute-done.18
  418.8 10.5 %collective-permute-done.19 = f32[2,384,128]{1,2,0:T(8,128)S(1)} collective-permute-done((f32[2,384,128]{1,2,0:T(8,128)S(1)}, f32[2,384,128]{1,2,0:T(8,128)S(1)}, u32[]{:S(2)}, u32[]{:S(2)}) %collective-permute-start.19) | collective-permute-done | bytes 393248 | tf_op jit(solution)/shard_map/ppermute | solution.py:20
  436.7 36.2 %all-reduce.25.cloned.1.call-done = f32[2,256,256]{2,1,0:T(8,128)} async-done(((f32[2,256,256]{2,1,0:T(8,128)}), f32[2,256,256]{2,1,0:T(8,128)}) %all-reduce.25.cloned.1.call-update) | async-done | bytes 524304 | tf_op jit(solution)/shard_map/psum | solution.py:156
  480.9 7.8 dynamic_update_slice.28
  490.7 8.2 %dynamic_update_slice.29 = f32[2,384,512]{1,2,0:T(8,128)S(1)} dynamic-update-slice(f32[2,384,512]{1,2,0:T(8,128)S(1)} %dynamic_update_slice.28, f32[2,256,256]{1,2,0:T(8,128)} %fusion.44, s32[]{:T(128)} %constant.15.clone.1, s32[]{:T(128)S(6)} %select_n.33, s32[]{:T(128)S(6)} %select_n.34) | dynamic-update-slice | bytes 1048580 | tf_op jit(solution)/shard_map/dynamic_update_slice | solution.py:167
  501.8 2.3 collective-permute-done.21
  504.2 3.3 collective-permute-start.22
  508.8 12.9 %collective-permute-done.22 = f32[2,640,128]{1,2,0:T(8,128)S(1)} collective-permute-done((f32[2,640,128]{1,2,0:T(8,128)S(1)}, f32[2,640,128]{1,2,0:T(8,128)S(1)}, u32[]{:S(2)}, u32[]{:S(2)}) %collective-permute-start.22) | collective-permute-done | bytes 655392 | tf_op jit(solution)/shard_map/ppermute | solution.py:17
  521.8 16.7 %collective-permute-done.23 = f32[2,640,128]{1,2,0:T(8,128)S(1)} collective-permute-done((f32[2,640,128]{1,2,0:T(8,128)S(1)}, f32[2,640,128]{1,2,0:T(8,128)S(1)}, u32[]{:S(2)}, u32[]{:S(2)}) %collective-permute-start.23) | collective-permute-done | bytes 655392 | tf_op jit(solution)/shard_map/ppermute | solution.py:20
  539.5 33.7 %all-reduce.27.cloned.1.call-done = f32[2,128,256]{1,2,0:T(8,128)} async-done(((f32[2,128,256]{1,2,0:T(8,128)}), f32[2,128,256]{1,2,0:T(8,128)}) %all-reduce.27.cloned.1.call-update) | async-done | bytes 262160 | tf_op jit(solution)/shard_map/psum | solution.py:159
  576.8 2.1 collective-permute-done.25
  579.0 3.4 collective-permute-start.26
  583.7 7.3 collective-permute-done.26
  591.1 10.3 %collective-permute-done.27 = f32[2,384,128]{1,2,0:T(8,128)S(1)} collective-permute-done((f32[2,384,128]{1,2,0:T(8,128)S(1)}, f32[2,384,128]{1,2,0:T(8,128)S(1)}, u32[]{:S(2)}, u32[]{:S(2)}) %collective-permute-start.27) | collective-permute-done | bytes 393248 | tf_op jit(solution)/shard_map/ppermute | solution.py:20
  609.1 37.7 %all-reduce.29.cloned.1.call-done = f32[2,256,256]{2,1,0:T(8,128)} async-done(((f32[2,256,256]{2,1,0:T(8,128)}), f32[2,256,256]{2,1,0:T(8,128)}) %all-reduce.29.cloned.1.call-update) | async-done | bytes 524304 | tf_op jit(solution)/shard_map/psum | solution.py:156
  654.4 8.2 %dynamic_update_slice.30 = f32[2,384,512]{1,2,0:T(8,128)S(1)} dynamic-update-slice(f32[2,384,512]{1,2,0:T(8,128)S(1)} %broadcast.214, f32[2,256,256]{1,2,0:T(8,128)S(1)} %fusion.25, s32[]{:T(128)} %constant.15.clone.1, s32[]{:T(128)S(6)} %select_n.31, s32[]{:T(128)S(6)} %select_n.32) | dynamic-update-slice | bytes 1048580 | tf_op jit(solution)/shard_map/dynamic_update_slice | solution.py:167
  663.8 8.8 %dynamic_update_slice.31 = f32[2,384,512]{1,2,0:T(8,128)S(1)} dynamic-update-slice(f32[2,384,512]{1,2,0:T(8,128)S(1)} %dynamic_update_slice.30, f32[2,256,256]{1,2,0:T(8,128)S(1)} %fusion.41, s32[]{:T(128)} %constant.15.clone.1, s32[]{:T(128)S(6)} %select_n.33, s32[]{:T(128)S(6)} %select_n.34) | dynamic-update-slice | bytes 1048580 | tf_op jit(solution)/shard_map/dynamic_update_slice | solution.py:167
  675.5 2.3 collective-permute-done.29
  678.0 3.2 collective-permute-start.30
  682.5 12.9 %collective-permute-done.30 = f32[2,640,128]{1,2,0:T(8,128)S(1)} collective-permute-done((f32[2,640,128]{1,2,0:T(8,128)S(1)}, f32[2,640,128]{1,2,0:T(8,128)S(1)}, u32[]{:S(2)}, u32[]{:S(2)}) %collective-permute-start.30) | collective-permute-done | bytes 655392 | tf_op jit(solution)/shard_map/ppermute | solution.py:17
  695.4 16.9 %collective-permute-done.31 = f32[2,640,128]{1,2,0:T(8,128)S(1)} collective-permute-done((f32[2,640,128]{1,2,0:T(8,128)S(1)}, f32[2,640,128]{1,2,0:T(8,128)S(1)}, u32[]{:S(2)}, u32[]{:S(2)}) %collective-permute-start.31) | collective-permute-done | bytes 655392 | tf_op jit(solution)/shard_map/ppermute | solution.py:20
  713.4 33.8 %all-reduce.31.cloned.1.call-done = f32[2,128,256]{1,2,0:T(8,128)} async-done(((f32[2,128,256]{1,2,0:T(8,128)}), f32[2,128,256]{1,2,0:T(8,128)}) %all-reduce.31.cloned.1.call-update) | async-done | bytes 262160 | tf_op jit(solution)/shard_map/psum | solution.py:159
  749.6 40.4 %all-reduce.6 = (f32[32]{0:T(128)S(1)}, f32[]{:T(128)}) all-reduce(f32[32]{0:T(128)S(1)} %dynamic-update-slice.1, f32[]{:T(128)} %get-tuple-element.13), channel_id=1, replica_groups=mesh['gx'=2,'gy'=4,'ma'=4] {'gx','gy','ma'}, use_global_device_ids=true, to_apply=%add.5 | all-reduce | flops 33 | bytes 264
  (254 shorter events, 122.8 us)
Async XLA Ops:
  6.5 75.0 %all-reduce.17.cloned.1.call-start = ((), (), s32[]{:S(2)}) async-start(), calls=%async_computation | async-start | bytes 1048576 | tf_op jit(solution)/shard_map/psum | solution.py:156
  6.5 5.2 collective-permute-start
  9.1 3.6 collective-permute-start.1
  13.7 17.1 %collective-permute-start.2 = (f32[2,384,128]{2,1,0:T(8,128)}, f32[2,384,128]{2,1,0:T(8,128)S(1)}, u32[]{:S(2)}, u32[]{:S(2)}) collective-permute-start(f32[2,384,128]{2,1,0:T(8,128)} %get-tuple-element.69), channel_id=1, source_target_pairs={{0,4},{4,8},{8,12},{1,5},{5,9},{9,13},{2,6},{6,10},{10,14},{3,7},{... | collective-permute-start | bytes 1179656 | tf_op jit(solution)/shard_map/ppermute | solution.py:17
  17.9 19.4 %collective-permute-start.3 = (f32[2,384,128]{2,1,0:T(8,128)}, f32[2,384,128]{2,1,0:T(8,128)}, u32[]{:S(2)}, u32[]{:S(2)}) collective-permute-start(f32[2,384,128]{2,1,0:T(8,128)} %get-tuple-element.70), channel_id=1, source_target_pairs={{4,0},{8,4},{12,8},{5,1},{9,5},{13,9},{6,2},{10,6},{14,10},{7,3},{... | collective-permute-start | bytes 1179656 | tf_op jit(solution)/shard_map/ppermute | solution.py:20
  28.1 10.3 %copy-start.18 = (bf16[512,512]{1,0:T(8,128)(2,1)}, bf16[512,512]{1,0:T(8,128)(2,1)S(1)}, u32[]{:S(2)}) copy-start(bf16[512,512]{1,0:T(8,128)(2,1)S(1)} %get-tuple-element.72) | copy-start | bytes 1572868
  28.2 11.4 %copy-start.27 = (bf16[2,256,2,256]{3,2,1,0:T(2,128)(2,1)}, bf16[2,256,2,256]{3,2,1,0:T(2,128)(2,1)S(1)}, u32[]{:S(2)}) copy-start(bf16[2,256,2,256]{3,2,1,0:T(2,128)(2,1)S(1)} %convert_element_type.132) | copy-start | bytes 1572868
  41.4 41.6 %copy-start = (f32[2,2,256,512,1]{3,2,4,1,0:T(8,128)}, f32[2,2,256,512,1]{3,2,4,1,0:T(8,128)S(1)}, u32[]{:S(2)}) copy-start(f32[2,2,256,512,1]{3,2,4,1,0:T(8,128)S(1)} %get-tuple-element.78) | copy-start | bytes 6291460
  42.5 139.8 %all-reduce.19.cloned.1.call-start = ((), (), s32[]{:S(2)}) async-start(), calls=%async_computation.1 | async-start | bytes 524288 | tf_op jit(solution)/shard_map/psum | solution.py:159
  107.7 2.8 collective-permute-start.4
  109.0 3.8 collective-permute-start.5
  112.9 17.5 %collective-permute-start.6 = (f32[2,640,128]{1,2,0:T(8,128)S(1)}, f32[2,640,128]{1,2,0:T(8,128)S(1)}, u32[]{:S(2)}, u32[]{:S(2)}) collective-permute-start(f32[2,640,128]{1,2,0:T(8,128)S(1)} %get-tuple-element.27), channel_id=1, source_target_pairs={{0,4},{4,8},{8,12},{1,5},{5,9},{9,13},{2,6},{6,10},{10,14},{3,7},{... | collective-permute-start | bytes 1966088 | tf_op jit(solution)/shard_map/ppermute | solution.py:17
  116.2 30.9 %collective-permute-start.7 = (f32[2,640,128]{1,2,0:T(8,128)S(1)}, f32[2,640,128]{1,2,0:T(8,128)S(1)}, u32[]{:S(2)}, u32[]{:S(2)}) collective-permute-start(f32[2,640,128]{1,2,0:T(8,128)S(1)} %get-tuple-element.28), channel_id=1, source_target_pairs={{4,0},{8,4},{12,8},{5,1},{9,5},{13,9},{6,2},{10,6},{14,10},{7,3},{... | collective-permute-start | bytes 1966088 | tf_op jit(solution)/shard_map/ppermute | solution.py:20
  148.6 107.5 %all-reduce.21.cloned.1.call-start = ((), (), s32[]{:S(2)}) async-start(), calls=%async_computation.2 | async-start | bytes 1048576 | tf_op jit(solution)/shard_map/psum | solution.py:156
  183.3 2.6 collective-permute-start.8
  184.6 3.4 collective-permute-start.9
  188.2 12.0 %collective-permute-start.10 = (f32[2,384,128]{1,2,0:T(8,128)S(1)}, f32[2,384,128]{1,2,0:T(8,128)S(1)}, u32[]{:S(2)}, u32[]{:S(2)}) collective-permute-start(f32[2,384,128]{1,2,0:T(8,128)S(1)} %get-tuple-element.67), channel_id=1, source_target_pairs={{0,4},{4,8},{8,12},{1,5},{5,9},{9,13},{2,6},{6,10},{10,14},{3,7},{... | collective-permute-start | bytes 1179656 | tf_op jit(solution)/shard_map/ppermute | solution.py:17
  191.6 19.0 %collective-permute-start.11 = (f32[2,384,128]{1,2,0:T(8,128)S(1)}, f32[2,384,128]{1,2,0:T(8,128)S(1)}, u32[]{:S(2)}, u32[]{:S(2)}) collective-permute-start(f32[2,384,128]{1,2,0:T(8,128)S(1)} %get-tuple-element.68), channel_id=1, source_target_pairs={{4,0},{8,4},{12,8},{5,1},{9,5},{13,9},{6,2},{10,6},{14,10},{7,3},{... | collective-permute-start | bytes 1179656 | tf_op jit(solution)/shard_map/ppermute | solution.py:20
  218.3 137.9 %all-reduce.23.cloned.1.call-start = ((), (), s32[]{:S(2)}) async-start(), calls=%async_computation.3 | async-start | bytes 524288 | tf_op jit(solution)/shard_map/psum | solution.py:159
  282.0 2.8 collective-permute-start.12
  283.3 3.8 collective-permute-start.13
  287.2 17.5 %collective-permute-start.14 = (f32[2,640,128]{1,2,0:T(8,128)S(1)}, f32[2,640,128]{1,2,0:T(8,128)S(1)}, u32[]{:S(2)}, u32[]{:S(2)}) collective-permute-start(f32[2,640,128]{1,2,0:T(8,128)S(1)} %get-tuple-element.25), channel_id=1, source_target_pairs={{0,4},{4,8},{8,12},{1,5},{5,9},{9,13},{2,6},{6,10},{10,14},{3,7},{... | collective-permute-start | bytes 1966088 | tf_op jit(solution)/shard_map/ppermute | solution.py:17
  290.5 30.9 %collective-permute-start.15 = (f32[2,640,128]{1,2,0:T(8,128)S(1)}, f32[2,640,128]{1,2,0:T(8,128)S(1)}, u32[]{:S(2)}, u32[]{:S(2)}) collective-permute-start(f32[2,640,128]{1,2,0:T(8,128)S(1)} %get-tuple-element.26), channel_id=1, source_target_pairs={{4,0},{8,4},{12,8},{5,1},{9,5},{13,9},{6,2},{10,6},{14,10},{7,3},{... | collective-permute-start | bytes 1966088 | tf_op jit(solution)/shard_map/ppermute | solution.py:20
  321.6 79.5 %copy-start.25 = (f32[2,128,256]{1,2,0:T(8,128)S(1)}, f32[2,128,256]{1,2,0:T(8,128)}, u32[]{:S(2)}) copy-start(f32[2,128,256]{1,2,0:T(8,128)} %all-reduce.19.cloned.1.call-done) | copy-start | bytes 786436
  322.4 150.5 %all-reduce.25.cloned.1.call-start = ((), (), s32[]{:S(2)}) async-start(), calls=%async_computation.4 | async-start | bytes 1048576 | tf_op jit(solution)/shard_map/psum | solution.py:156
  401.1 28.2 %copy-start.16 = (f32[2,128,256]{1,2,0:T(8,128)}, f32[2,128,256]{1,2,0:T(8,128)S(1)}, u32[]{:S(2)}) copy-start(f32[2,128,256]{1,2,0:T(8,128)S(1)} %multiply_add_fusion.1) | copy-start | bytes 786436
  401.1 2.6 collective-permute-start.16
  402.4 3.4 collective-permute-start.17
  405.9 12.8 %collective-permute-start.18 = (f32[2,384,128]{1,2,0:T(8,128)S(1)}, f32[2,384,128]{1,2,0:T(8,128)S(1)}, u32[]{:S(2)}, u32[]{:S(2)}) collective-permute-start(f32[2,384,128]{1,2,0:T(8,128)S(1)} %get-tuple-element.65), channel_id=1, source_target_pairs={{0,4},{4,8},{8,12},{1,5},{5,9},{9,13},{2,6},{6,10},{10,14},{3,7},{... | collective-permute-start | bytes 1179656 | tf_op jit(solution)/shard_map/ppermute | solution.py:17
  410.2 19.2 %collective-permute-start.19 = (f32[2,384,128]{1,2,0:T(8,128)S(1)}, f32[2,384,128]{1,2,0:T(8,128)S(1)}, u32[]{:S(2)}, u32[]{:S(2)}) collective-permute-start(f32[2,384,128]{1,2,0:T(8,128)S(1)} %get-tuple-element.66), channel_id=1, source_target_pairs={{4,0},{8,4},{12,8},{5,1},{9,5},{13,9},{6,2},{10,6},{14,10},{7,3},{... | collective-permute-start | bytes 1179656 | tf_op jit(solution)/shard_map/ppermute | solution.py:20
  435.3 39.0 %copy-start.2 = (f32[2,2,256,512,1]{3,2,4,1,0:T(8,128)}, f32[2,2,256,512,1]{3,2,4,1,0:T(8,128)S(1)}, u32[]{:S(2)}) copy-start(f32[2,2,256,512,1]{3,2,4,1,0:T(8,128)S(1)} %get-tuple-element.80) | copy-start | bytes 6291460
  436.4 136.8 %all-reduce.27.cloned.1.call-start = ((), (), s32[]{:S(2)}) async-start(), calls=%async_computation.5 | async-start | bytes 524288 | tf_op jit(solution)/shard_map/psum | solution.py:159
  499.0 2.8 collective-permute-start.20
  500.3 3.8 collective-permute-start.21
  504.2 17.5 %collective-permute-start.22 = (f32[2,640,128]{1,2,0:T(8,128)S(1)}, f32[2,640,128]{1,2,0:T(8,128)S(1)}, u32[]{:S(2)}, u32[]{:S(2)}) collective-permute-start(f32[2,640,128]{1,2,0:T(8,128)S(1)} %get-tuple-element.23), channel_id=1, source_target_pairs={{0,4},{4,8},{8,12},{1,5},{5,9},{9,13},{2,6},{6,10},{10,14},{3,7},{... | collective-permute-start | bytes 1966088 | tf_op jit(solution)/shard_map/ppermute | solution.py:17
  507.5 30.9 %collective-permute-start.23 = (f32[2,640,128]{1,2,0:T(8,128)S(1)}, f32[2,640,128]{1,2,0:T(8,128)S(1)}, u32[]{:S(2)}, u32[]{:S(2)}) collective-permute-start(f32[2,640,128]{1,2,0:T(8,128)S(1)} %get-tuple-element.24), channel_id=1, source_target_pairs={{4,0},{8,4},{12,8},{5,1},{9,5},{13,9},{6,2},{10,6},{14,10},{7,3},{... | collective-permute-start | bytes 1966088 | tf_op jit(solution)/shard_map/ppermute | solution.py:20
  539.4 107.4 %all-reduce.29.cloned.1.call-start = ((), (), s32[]{:S(2)}) async-start(), calls=%async_computation.6 | async-start | bytes 1048576 | tf_op jit(solution)/shard_map/psum | solution.py:156
  574.2 2.6 collective-permute-start.24
  575.5 3.4 collective-permute-start.25
  579.0 12.0 %collective-permute-start.26 = (f32[2,384,128]{1,2,0:T(8,128)S(1)}, f32[2,384,128]{1,2,0:T(8,128)S(1)}, u32[]{:S(2)}, u32[]{:S(2)}) collective-permute-start(f32[2,384,128]{1,2,0:T(8,128)S(1)} %get-tuple-element.63), channel_id=1, source_target_pairs={{0,4},{4,8},{8,12},{1,5},{5,9},{9,13},{2,6},{6,10},{10,14},{3,7},{... | collective-permute-start | bytes 1179656 | tf_op jit(solution)/shard_map/ppermute | solution.py:17
  582.4 19.0 %collective-permute-start.27 = (f32[2,384,128]{1,2,0:T(8,128)S(1)}, f32[2,384,128]{1,2,0:T(8,128)S(1)}, u32[]{:S(2)}, u32[]{:S(2)}) collective-permute-start(f32[2,384,128]{1,2,0:T(8,128)S(1)} %get-tuple-element.64), channel_id=1, source_target_pairs={{4,0},{8,4},{12,8},{5,1},{9,5},{13,9},{6,2},{10,6},{14,10},{7,3},{... | collective-permute-start | bytes 1179656 | tf_op jit(solution)/shard_map/ppermute | solution.py:20
  609.1 138.0 %all-reduce.31.cloned.1.call-start = ((), (), s32[]{:S(2)}) async-start(), calls=%async_computation.7 | async-start | bytes 524288 | tf_op jit(solution)/shard_map/psum | solution.py:159
  672.7 2.8 collective-permute-start.28
  674.1 3.8 collective-permute-start.29
  678.0 17.5 %collective-permute-start.30 = (f32[2,640,128]{1,2,0:T(8,128)S(1)}, f32[2,640,128]{1,2,0:T(8,128)S(1)}, u32[]{:S(2)}, u32[]{:S(2)}) collective-permute-start(f32[2,640,128]{1,2,0:T(8,128)S(1)} %get-tuple-element.21), channel_id=1, source_target_pairs={{0,4},{4,8},{8,12},{1,5},{5,9},{9,13},{2,6},{6,10},{10,14},{3,7},{... | collective-permute-start | bytes 1966088 | tf_op jit(solution)/shard_map/ppermute | solution.py:17
  681.2 31.1 %collective-permute-start.31 = (f32[2,640,128]{1,2,0:T(8,128)S(1)}, f32[2,640,128]{1,2,0:T(8,128)S(1)}, u32[]{:S(2)}, u32[]{:S(2)}) collective-permute-start(f32[2,640,128]{1,2,0:T(8,128)S(1)} %get-tuple-element.22), channel_id=1, source_target_pairs={{4,0},{8,4},{12,8},{5,1},{9,5},{13,9},{6,2},{10,6},{14,10},{7,3},{... | collective-permute-start | bytes 1966088 | tf_op jit(solution)/shard_map/ppermute | solution.py:20
  712.5 79.4 %copy-start.17 = (f32[2,128,256]{1,2,0:T(8,128)S(1)}, f32[2,128,256]{1,2,0:T(8,128)}, u32[]{:S(2)}) copy-start(f32[2,128,256]{1,2,0:T(8,128)} %copy-done.16) | copy-start | bytes 786436
  712.5 79.4 %copy-start.26 = (f32[2,128,256]{1,2,0:T(8,128)S(1)}, f32[2,128,256]{1,2,0:T(8,128)}, u32[]{:S(2)}) copy-start(f32[2,128,256]{1,2,0:T(8,128)} %all-reduce.27.cloned.1.call-done) | copy-start | bytes 786436
  (25 other events, 40.3 us)
Sparse Core Ops, SparseCore 0:
  42.6 38.8 all-reduce.16
  148.7 33.5 all-reduce.18
  218.4 37.6 all-reduce.20
  322.5 33.5 all-reduce.22
  436.6 36.3 all-reduce.24
  539.6 33.5 all-reduce.26
  609.2 37.6 all-reduce.28
  713.5 33.5 all-reduce.30
